TPU v7x, 32 devices: a whole 2x2x4 slice. The times are simulated.
32 devices in a mesh: dp: 2 (over y), mp: 16 (over z, x, core).
Axes of the slice: x: 2, y: 2, z: 4, core: 2. Of those that a mesh axis runs over, the one named last changes fastest.
Arguments:
- features: bfloat16 [32, 1280, 1024], P('dp', 'mp'), may hold values from -6 to 6
- conv_weight: bfloat16 [1280, 1280], P('mp'), may hold values from -0.15625 to 0.15625
- norm_gain: float32 [1280], replicated, may hold values from 0.25 to 1.75
- norm_bias: float32 [1280], replicated, may hold values from -3 to 3
- logit_vector: float32 [1280], replicated, may hold values from -0.625 to 0.625
- labels: int32 [32], P(('dp', 'mp')), may hold values 0 or 1
Outputs:
- grad_features: float32 [32, 1280, 1024], P('dp', 'mp')
- grad_weight: float32 [1280, 1280], P('mp')
- head_grads: float32 [3, 1280], replicated
- loss: float32 [], replicated
All inputs are finite; a program needn't handle non-finite values. No bound on the sum of `labels` on one device may be relied on, other than what follows from the above.
Results may differ from a plain program's by a relative error of at most 0.0029.
Values may be sent and summed in bfloat16 or wider, within the bound.
No kernel may reach another device: no remote copies, remote signals or barrier semaphores. Data moves between devices by JAX's collectives and lax.ppermute only.
A program may use at most 128 MiB of HBM per device.

v0:
```python
import jax
import jax.numpy as jnp
from jax import lax
from jax.sharding import PartitionSpec as P

GROUPS = 32
norm_eps = 1e-05


def head_total(pre, norm_gain, norm_bias, logit_vector, signs):
    images, channels, cell_count = pre.shape
    grouped = pre.reshape(images, GROUPS, channels // GROUPS, cell_count)
    center = jnp.mean(grouped, axis=(2, 3), keepdims=True)
    spread = jnp.mean((grouped - center) ** 2, axis=(2, 3), keepdims=True)
    normed = ((grouped - center) * lax.rsqrt(spread + norm_eps)).reshape(
        images, channels, cell_count
    )
    normed = normed * norm_gain[:, None] + norm_bias[:, None]
    hidden = jax.nn.silu(normed)
    logits = (
        jnp.einsum("c,ncs->n", logit_vector, hidden, precision=lax.Precision.HIGHEST) / cell_count
    )
    margin = jnp.maximum(1.0 - signs * logits, 0.0)
    return jnp.sum(margin * margin)


def shards(features, conv_weight, norm_gain, norm_bias, logit_vector, labels):
    signs = 2.0 * labels.astype(jnp.float32) - 1.0
    weight_full = lax.all_gather(conv_weight, "mp", axis=0, tiled=True)
    image_block = lax.all_to_all(features, "mp", split_axis=0, concat_axis=1, tiled=True)
    pre = jnp.einsum("io,nis->nos", weight_full, image_block, preferred_element_type=jnp.float32)
    total, pull = jax.vjp(
        lambda p, g, b, h: head_total(p, g, b, h, signs), pre, norm_gain, norm_bias, logit_vector
    )
    grad_pre, grad_gain, grad_bias, grad_vec = pull(jnp.ones((), jnp.float32))
    grad_pre = grad_pre.astype(jnp.bfloat16)
    grad_image = jnp.einsum(
        "io,nos->nis", weight_full, grad_pre, preferred_element_type=jnp.float32
    )
    grad_features = lax.all_to_all(grad_image, "mp", split_axis=1, concat_axis=0, tiled=True)
    weight_term = jnp.einsum(
        "nis,nos->io", image_block, grad_pre, preferred_element_type=jnp.float32
    )
    summed = lax.psum(weight_term, "dp")
    grad_weight = lax.psum_scatter(summed, "mp", scatter_dimension=0, tiled=True)
    total_sum, head_grads = lax.psum(
        (total, jnp.stack([grad_gain, grad_bias, grad_vec])), ("dp", "mp")
    )
    image_total = pre.shape[0] * lax.axis_size("dp") * lax.axis_size("mp")
    loss = total_sum / image_total
    return (grad_features, grad_weight, head_grads, loss)


def solution(mesh):
    return jax.shard_map(
        shards,
        mesh=mesh,
        in_specs=(P("dp", "mp", None), P("mp", None), P(), P(), P(), P(("dp", "mp"))),
        out_specs=(P("dp", "mp", None), P("mp", None), P(), P()),
        check_vma=False,
    )
```

profile of v0, /device:TPU:12, one launch (start us, length us, event | category | flops | bytes accessed | tf_op | source)
XLA Modules:
  0.0 369.9 jit_solution(1314709763259043762)
XLA Ops:
  7.2 0.0 all-gather.2.cloned.1.call-start
  7.2 0.7 all-gather.2.cloned.1.call-update
  7.9 6.3 %all-to-all-start = ((bf16[16,80,1024]{2,1,0:T(8,128)(2,1)}), bf16[16,80,1024]{2,1,0:T(8,128)(2,1)S(1)}, u32[]{:S(2)}, u32[]{:S(2)}) async-start(bf16[16,80,1024]{2,1,0:T(8,128)(2,1)} %param.6), calls=%async_computation | async-start | bytes 5242880 | tf_op jit(solution)/shard_map/all_to_all | solution.py:30
  14.2 0.0 reduce-scatter.4.cloned.1.call-start
  14.9 76.1 %all-to-all-done = bf16[16,80,1024]{2,1,0:T(8,128)(2,1)S(1)} async-done(((bf16[16,80,1024]{2,1,0:T(8,128)(2,1)}), bf16[16,80,1024]{2,1,0:T(8,128)(2,1)S(1)}, u32[]{:S(2)}, u32[]{:S(2)}) %all-to-all-start) | async-done | bytes 2621472 | tf_op jit(solution)/shard_map/all_to_all | solution.py:30
  91.0 0.0 all-gather.2.cloned.1.call-done
  91.0 7.3 %fusion.10 = (f32[1280]{0:T(1024)S(1)}, f32[1024,1280]{1,0:T(8,128)}) fusion(bf16[1280,1024]{1,0:T(8,128)(2,1)S(1)} %bitcast.86, bf16[1280,1280]{1,0:T(8,128)(2,1)} %all-gather.2.cloned.1.call-done), kind=kOutput, calls=%fused_computation.30 | convolution fusion | flops 3356752640 | bytes 11146240 | tf_op jit(solution)/shard_map/io,nis->nos/dot_general | solution.py:31
  98.3 0.0 copy-start
  98.3 0.0 copy-start.1
  98.3 0.1 reduce_sum.138
  98.4 0.1 reduce_sum.139
  98.5 0.1 sub.52
  98.6 0.1 sub.53
  98.7 0.0 copy-start.2
  98.7 3.1 fusion.2
  101.8 0.1 reduce_sum.141
  101.9 0.1 reduce_sum.142
  102.0 0.1 mul.155
  102.1 0.1 mul.156
  102.2 0.0 copy-done
  102.2 0.0 copy-done.1
  102.2 4.2 %multiply_reduce_fusion.1 = f32[1280]{0:T(1024)S(1)} fusion(f32[1024,1280]{1,0:T(8,128)} %get-tuple-element.27, f32[1280]{0:T(1024)S(1)} %copy-done, f32[1280]{0:T(1024)S(1)} %copy-done.1, f32[1280]{0:T(1024)S(1)} %mul.156, f32[1280]{0:T(1024)S(1)} %sub.53), kind=kLoop, calls=%fused_computation.13 | loop fusion | flops 11795200 | bytes 5268480 | tf_op jit(solution)/shard_map/jvp(c,ncs->n)/reduce_sum | solution.py:21
  106.4 0.0 copy-done.2
  106.4 0.6 multiply_reduce_fusion.3
  107.7 5.7 %multiply_reduce_fusion = (f32[1280]{0:T(1024)S(1)}, f32[1280]{0:T(1024)S(1)}, f32[1280]{0:T(1024)S(1)}, f32[1280]{0:T(1024)S(1)}) fusion(f32[1024,1280]{1,0:T(8,128)} %get-tuple-element.27, f32[1280]{0:T(1024)S(1)} %mul.156, f32[1280]{0:T(1024)S(1)} %sub.53, f32[1280]{0:T(1024)S(1)} %copy-done, f32[1280]{0:T(1024)S(1)} %copy-done.1, ...), kind=kLoop, calls=%fused_computation.11 | loop fusion | flops 27520000 | bytes 5288960 | tf_op jit(solution)/shard_map/transpose(jvp())/reduce_sum | solution.py:18
  113.4 0.1 reduce_sum.148
  113.5 0.1 reduce_sum.149
  113.6 0.1 reduce_sum.145
  113.7 0.1 reduce_sum.146
  113.8 0.1 mul.177
  113.9 0.1 mul.178
  114.0 3.1 fusion.4
  117.1 0.1 reduce_sum.151
  117.2 0.1 reduce_sum.152
  117.3 0.1 broadcast_in_dim.9
  117.4 0.1 broadcast_in_dim.10
  117.5 11.6 %convolution_bitcast_fusion = f32[1280,1280]{0,1:T(8,128)} fusion(bf16[1280,1024]{1,0:T(8,128)(2,1)S(1)} %bitcast.87, f32[1024,1280]{1,0:T(8,128)} %get-tuple-element.27, f32[1280]{0:T(1024)S(1)} %broadcast_in_dim.10, f32[1280]{0:T(1024)S(1)} %mul.178, f32[1280]{0:T(1024)S(1)} %copy-done.1, f32[1280]{0:T(1024)S(1)} %mul.156, f32[1280]{0:T(1024)S(1)} %sub.53, ...), kind=kOutput, calls=%fused_computation | convolution fusion | flops 3380346880 | bytes 14453760 | tf_op jit(solution)/shard_map/nis,nos->io/dot_general | solution.py:41
  129.1 8.2 %copy.20 = f32[1280,1280]{1,0:T(8,128)} copy(f32[1280,1280]{0,1:T(8,128)} %convolution_bitcast_fusion) | data formatting | bytes 13107200
  137.3 0.0 reduce-scatter.4.cloned.1.call-update
  137.3 12.1 %convolution_bitcast_fusion.1 = f32[1,1280,1024]{1,2,0:T(8,128)} fusion(bf16[1280,1280]{1,0:T(8,128)(2,1)} %all-gather.2.cloned.1.call-done, f32[1024,1280]{1,0:T(8,128)} %get-tuple-element.27, f32[1280]{0:T(1024)S(1)} %broadcast_in_dim.10, f32[1280]{0:T(1024)S(1)} %mul.178, f32[1280]{0:T(1024)S(1)} %copy-done.1, f32[1280]{0:T(1024)S(1)} %mul.156, ...), kind=kOutput, calls=%fused_computation.18 | convolution fusion | flops 3380346880 | bytes 13798400 | tf_op jit(solution)/shard_map/io,nos->nis/dot_general | solution.py:37
  149.4 11.9 %copy.16 = f32[1,1280,1024]{2,0,1:T(1,128)} copy(f32[1,1280,1024]{1,2,0:T(8,128)} %convolution_bitcast_fusion.1) | data formatting | bytes 10485760 | tf_op jit(solution)/shard_map/io,nos->nis/transpose | solution.py:37
  161.3 6.4 %all-to-all-start.1 = ((f32[1,1280,1024]{2,0,1:T(1,128)}), f32[1,1280,1024]{2,0,1:T(1,128)}, u32[]{:S(2)}, u32[]{:S(2)}) async-start(f32[1,1280,1024]{2,0,1:T(1,128)} %copy.16), calls=%async_computation.1 | async-start | bytes 10485760 | tf_op jit(solution)/shard_map/all_to_all | solution.py:40
  167.7 0.0 all-reduce.3.cloned.1.call-start
  167.7 133.2 %reduce-scatter.4.cloned.1.call-done = f32[80,1280]{1,0:T(8,128)} async-done(((f32[1280,1280]{1,0:T(8,128)}), f32[80,1280]{1,0:T(8,128)}) %reduce-scatter.4.cloned.1.call-update) | async-done | bytes 409616
  300.9 2.1 copy.21
  302.9 0.0 all-reduce.3.cloned.1.call-update
  303.1 50.3 %all-reduce = (f32[3,1280]{1,0:T(4,128)}, f32[]{:T(128)}) all-reduce(f32[3,1280]{1,0:T(4,128)S(1)} %pad_maximum_fusion, f32[]{:T(128)} %bitcast.9), channel_id=1, replica_groups=mesh['dp'=2,'mp'=16] {'dp','mp'}, use_global_device_ids=true, to_apply=%region_15.16 | all-reduce | flops 3841 | bytes 30728 | tf_op jit(solution)/shard_map/psum | solution.py:46
  354.0 0.0 all-to-all-done.1
  354.0 6.1 %copy.22 = f32[1,1280,1024]{2,1,0:T(8,128)} copy(f32[1,1280,1024]{2,0,1:T(1,128)} %all-to-all-done.1) | data formatting | bytes 10485760
  360.2 0.0 all-reduce.3.cloned.1.call-done
  360.2 2.1 copy.17
  (10 shorter events, 0.1 us)
Async XLA Ops:
  7.2 83.9 %all-gather.2.cloned.1.call-start = ((), (), s32[]{:S(2)}) async-start(), calls=%async_computation.3 | async-start | bytes 3481600 | tf_op jit(solution)/shard_map/all_gather | solution.py:29
  7.9 83.1 %all-to-all-start = ((bf16[16,80,1024]{2,1,0:T(8,128)(2,1)}), bf16[16,80,1024]{2,1,0:T(8,128)(2,1)S(1)}, u32[]{:S(2)}, u32[]{:S(2)}) async-start(bf16[16,80,1024]{2,1,0:T(8,128)(2,1)} %param.6), calls=%async_computation | async-start | bytes 5242880 | tf_op jit(solution)/shard_map/all_to_all | solution.py:30
  14.2 286.7 %reduce-scatter.4.cloned.1.call-start = ((), (), s32[]{:S(2)}) async-start(), calls=%async_computation.5 | async-start | bytes 6963200
  98.3 3.9 %copy-start = (f32[1280]{0:T(1024)S(1)}, f32[1280]{0:T(1024)}, u32[]{:S(2)}) copy-start(f32[1280]{0:T(1024)} %param.9) | copy-start | bytes 15364
  98.3 3.9 %copy-start.1 = (f32[1280]{0:T(1024)S(1)}, f32[1280]{0:T(1024)}, u32[]{:S(2)}) copy-start(f32[1280]{0:T(1024)} %param.8) | copy-start | bytes 15364
  98.7 7.7 %copy-start.2 = (f32[1280]{0:T(1024)S(1)}, f32[1280]{0:T(1024)}, u32[]{:S(2)}) copy-start(f32[1280]{0:T(1024)} %param.10) | copy-start | bytes 15364
  161.3 192.7 %all-to-all-start.1 = ((f32[1,1280,1024]{2,0,1:T(1,128)}), f32[1,1280,1024]{2,0,1:T(1,128)}, u32[]{:S(2)}, u32[]{:S(2)}) async-start(f32[1,1280,1024]{2,0,1:T(1,128)} %copy.16), calls=%async_computation.1 | async-start | bytes 10485760 | tf_op jit(solution)/shard_map/all_to_all | solution.py:40
  167.7 192.5 %all-reduce.3.cloned.1.call-start = ((), (), s32[]{:S(2)}) async-start(), calls=%async_computation.4 | async-start | bytes 1310720 | tf_op jit(solution)/shard_map/psum | solution.py:44
Sparse Core Ops, SparseCore 0:
  10.3 75.0 all-gather.1
  137.4 163.3 reduce-scatter.3
  303.2 30.7 all-reduce.2
where the time goes:
time: 371 us; the launch traced here: 370 us
  waiting for transfers between devices  210 us (57%)
  blocking collectives  50.3 us (14%)
  local copies, waits for them, and re-layouts  31.4 us (8%)
  matrix products  31.1 us (8%)
  other arithmetic  17.3 us (5%)
  between operations  17 us (5%)
  starting transfers between devices  12.8 us (3%)
    unnamed x4, waiting for transfers between devices  134 us
    all_to_all x1, waiting for transfers between devices, shards(): lax.all_to_all(features, 'mp', split_axis=0, concat_axis=1, tiled=True)  76.1 us
    psum x1, blocking collectives, shards(): lax.psum((total, jnp.stack([grad_gain, grad_bias, grad_vec])), ('dp', 'mp'))  50.3 us
    unnamed x10, local copies, waits for them, and re-layouts  18.4 us
    dot_general x1, matrix products, shards(): jnp.einsum('io,nos->nis', weight_full, grad_pre, preferred_element_type=j...  12.1 us
    transpose x1, local copies, waits for them, and re-layouts, shards(): jnp.einsum('io,nos->nis', weight_full, grad_pre, preferred_element_type=j...  11.9 us
    dot_general x1, matrix products, shards(): jnp.einsum('nis,nos->io', image_block, grad_pre, preferred_element_type=j...  11.6 us
  transfers between devices with their start and end apart: 5, of which 2 were waited for; matrix products, arithmetic and copies ran while one was open for 9% of the time, Pallas kernels for 0%

commit v1 on v0

--- a/solution.py
+++ b/solution.py
@@ -44,7 +44,7 @@
     summed = lax.psum(weight_term, "dp")
     grad_weight = lax.psum_scatter(summed, "mp", scatter_dimension=0, tiled=True)
     total_sum, head_grads = lax.psum(
-        (total, jnp.stack([grad_gain, grad_bias, grad_vec])), ("dp", "mp")
+        lax.psum((total, jnp.stack([grad_gain, grad_bias, grad_vec])), "mp"), "dp"
     )
     image_total = pre.shape[0] * lax.axis_size("dp") * lax.axis_size("mp")
     loss = total_sum / image_total

time: 371 us -> 390 us (1.051); the launches traced: 370 us -> 383 us
  blocking collectives: 50.3 us -> 63.5 us
    psum x1 -> x2, blocking collectives: 50.3 us -> 63.5 us  [the longest x1 55.1 us: shards(): lax.psum((total, jnp.stack([grad_gain, grad_bias, grad_vec])), 'mp')]
  transfers between devices with their start and end apart: 5 -> 5, of which waited for: 2 -> 2; matrix products, arithmetic and copies ran while one was open for 9% -> 8% of each run, Pallas kernels for 0% -> 0%
where the time goes in v1:
time: 390 us; the launch traced here: 383 us
  waiting for transfers between devices  210 us (54%)
  blocking collectives  63.5 us (16%)
  local copies, waits for them, and re-layouts  31.4 us (8%)
  matrix products  31.1 us (8%)
  other arithmetic  17.3 us (4%)
  between operations  17 us (4%)
  starting transfers between devices  12.8 us (3%)
    unnamed x4, waiting for transfers between devices  134 us
    all_to_all x1, waiting for transfers between devices, shards(): lax.all_to_all(features, 'mp', split_axis=0, concat_axis=1, tiled=True)  76.1 us
    psum x1, blocking collectives, shards(): lax.psum((total, jnp.stack([grad_gain, grad_bias, grad_vec])), 'mp')  55.1 us
    unnamed x10, local copies, waits for them, and re-layouts  18.4 us
    dot_general x1, matrix products, shards(): jnp.einsum('io,nos->nis', weight_full, grad_pre, preferred_element_type=j...  12.1 us
    transpose x1, local copies, waits for them, and re-layouts, shards(): jnp.einsum('io,nos->nis', weight_full, grad_pre, preferred_element_type=j...  11.9 us
    dot_general x1, matrix products, shards(): jnp.einsum('nis,nos->io', image_block, grad_pre, preferred_element_type=j...  11.6 us
    psum x1, blocking collectives, shards(): lax.psum(lax.psum((total, jnp.stack([grad_gain, grad_bias, grad_vec])), '...  8.42 us
  transfers between devices with their start and end apart: 5, of which 2 were waited for; matrix products, arithmetic and copies ran while one was open for 8% of the time, Pallas kernels for 0%

profile of v1, /device:TPU:12, one launch (start us, length us, event | category | flops | bytes accessed | tf_op | source)
XLA Modules:
  0.0 383.1 jit_solution(6290655433045862350)
XLA Ops:
  7.2 0.0 all-gather.2.cloned.1.call-start
  7.2 0.7 all-gather.2.cloned.1.call-update
  7.9 6.3 %all-to-all-start = ((bf16[16,80,1024]{2,1,0:T(8,128)(2,1)}), bf16[16,80,1024]{2,1,0:T(8,128)(2,1)S(1)}, u32[]{:S(2)}, u32[]{:S(2)}) async-start(bf16[16,80,1024]{2,1,0:T(8,128)(2,1)} %param.6), calls=%async_computation | async-start | bytes 5242880 | tf_op jit(solution)/shard_map/all_to_all | solution.py:30
  14.2 0.0 reduce-scatter.4.cloned.1.call-start
  14.9 76.1 %all-to-all-done = bf16[16,80,1024]{2,1,0:T(8,128)(2,1)S(1)} async-done(((bf16[16,80,1024]{2,1,0:T(8,128)(2,1)}), bf16[16,80,1024]{2,1,0:T(8,128)(2,1)S(1)}, u32[]{:S(2)}, u32[]{:S(2)}) %all-to-all-start) | async-done | bytes 2621472 | tf_op jit(solution)/shard_map/all_to_all | solution.py:30
  91.0 0.0 all-gather.2.cloned.1.call-done
  91.0 7.3 %fusion.10 = (f32[1280]{0:T(1024)S(1)}, f32[1024,1280]{1,0:T(8,128)}) fusion(bf16[1280,1024]{1,0:T(8,128)(2,1)S(1)} %bitcast.86, bf16[1280,1280]{1,0:T(8,128)(2,1)} %all-gather.2.cloned.1.call-done), kind=kOutput, calls=%fused_computation.30 | convolution fusion | flops 3356752640 | bytes 11146240 | tf_op jit(solution)/shard_map/io,nis->nos/dot_general | solution.py:31
  98.3 0.0 copy-start
  98.3 0.0 copy-start.1
  98.3 0.1 reduce_sum.138
  98.4 0.1 reduce_sum.139
  98.5 0.1 sub.52
  98.6 0.1 sub.53
  98.7 0.0 copy-start.2
  98.7 3.1 fusion.2
  101.8 0.1 reduce_sum.141
  101.9 0.1 reduce_sum.142
  102.0 0.1 mul.155
  102.1 0.1 mul.156
  102.2 0.0 copy-done
  102.2 0.0 copy-done.1
  102.2 4.2 %multiply_reduce_fusion.1 = f32[1280]{0:T(1024)S(1)} fusion(f32[1024,1280]{1,0:T(8,128)} %get-tuple-element.29, f32[1280]{0:T(1024)S(1)} %copy-done, f32[1280]{0:T(1024)S(1)} %copy-done.1, f32[1280]{0:T(1024)S(1)} %mul.156, f32[1280]{0:T(1024)S(1)} %sub.53), kind=kLoop, calls=%fused_computation.13 | loop fusion | flops 11795200 | bytes 5268480 | tf_op jit(solution)/shard_map/jvp(c,ncs->n)/reduce_sum | solution.py:21
  106.4 0.0 copy-done.2
  106.4 0.6 multiply_reduce_fusion.3
  107.7 5.7 %multiply_reduce_fusion = (f32[1280]{0:T(1024)S(1)}, f32[1280]{0:T(1024)S(1)}, f32[1280]{0:T(1024)S(1)}, f32[1280]{0:T(1024)S(1)}) fusion(f32[1024,1280]{1,0:T(8,128)} %get-tuple-element.29, f32[1280]{0:T(1024)S(1)} %mul.156, f32[1280]{0:T(1024)S(1)} %sub.53, f32[1280]{0:T(1024)S(1)} %copy-done, f32[1280]{0:T(1024)S(1)} %copy-done.1, ...), kind=kLoop, calls=%fused_computation.11 | loop fusion | flops 27520000 | bytes 5288960 | tf_op jit(solution)/shard_map/transpose(jvp())/reduce_sum | solution.py:18
  113.4 0.1 reduce_sum.148
  113.5 0.1 reduce_sum.149
  113.6 0.1 reduce_sum.145
  113.7 0.1 reduce_sum.146
  113.8 0.1 mul.177
  113.9 0.1 mul.178
  114.0 3.1 fusion.4
  117.1 0.1 reduce_sum.151
  117.2 0.1 reduce_sum.152
  117.3 0.1 broadcast_in_dim.9
  117.4 0.1 broadcast_in_dim.10
  117.5 11.6 %convolution_bitcast_fusion = f32[1280,1280]{0,1:T(8,128)} fusion(bf16[1280,1024]{1,0:T(8,128)(2,1)S(1)} %bitcast.87, f32[1024,1280]{1,0:T(8,128)} %get-tuple-element.29, f32[1280]{0:T(1024)S(1)} %broadcast_in_dim.10, f32[1280]{0:T(1024)S(1)} %mul.178, f32[1280]{0:T(1024)S(1)} %copy-done.1, f32[1280]{0:T(1024)S(1)} %mul.156, f32[1280]{0:T(1024)S(1)} %sub.53, ...), kind=kOutput, calls=%fused_computation | convolution fusion | flops 3380346880 | bytes 14453760 | tf_op jit(solution)/shard_map/nis,nos->io/dot_general | solution.py:41
  129.1 8.2 %copy.20 = f32[1280,1280]{1,0:T(8,128)} copy(f32[1280,1280]{0,1:T(8,128)} %convolution_bitcast_fusion) | data formatting | bytes 13107200
  137.3 0.0 reduce-scatter.4.cloned.1.call-update
  137.3 12.1 %convolution_bitcast_fusion.1 = f32[1,1280,1024]{1,2,0:T(8,128)} fusion(bf16[1280,1280]{1,0:T(8,128)(2,1)} %all-gather.2.cloned.1.call-done, f32[1024,1280]{1,0:T(8,128)} %get-tuple-element.29, f32[1280]{0:T(1024)S(1)} %broadcast_in_dim.10, f32[1280]{0:T(1024)S(1)} %mul.178, f32[1280]{0:T(1024)S(1)} %copy-done.1, f32[1280]{0:T(1024)S(1)} %mul.156, ...), kind=kOutput, calls=%fused_computation.18 | convolution fusion | flops 3380346880 | bytes 13798400 | tf_op jit(solution)/shard_map/io,nos->nis/dot_general | solution.py:37
  149.4 11.9 %copy.16 = f32[1,1280,1024]{2,0,1:T(1,128)} copy(f32[1,1280,1024]{1,2,0:T(8,128)} %convolution_bitcast_fusion.1) | data formatting | bytes 10485760 | tf_op jit(solution)/shard_map/io,nos->nis/transpose | solution.py:37
  161.3 6.4 %all-to-all-start.1 = ((f32[1,1280,1024]{2,0,1:T(1,128)}), f32[1,1280,1024]{2,0,1:T(1,128)}, u32[]{:S(2)}, u32[]{:S(2)}) async-start(f32[1,1280,1024]{2,0,1:T(1,128)} %copy.16), calls=%async_computation.1 | async-start | bytes 10485760 | tf_op jit(solution)/shard_map/all_to_all | solution.py:40
  167.7 0.0 all-reduce.4.cloned.1.call-start
  167.7 133.2 %reduce-scatter.4.cloned.1.call-done = f32[80,1280]{1,0:T(8,128)} async-done(((f32[1280,1280]{1,0:T(8,128)}), f32[80,1280]{1,0:T(8,128)}) %reduce-scatter.4.cloned.1.call-update) | async-done | bytes 409616
  300.9 2.1 copy.21
  302.9 0.0 all-reduce.4.cloned.1.call-update
  303.1 55.1 %all-reduce = (f32[3,1280]{1,0:T(4,128)S(1)}, f32[]{:T(128)}) all-reduce(f32[3,1280]{1,0:T(4,128)S(1)} %pad_maximum_fusion, f32[]{:T(128)} %bitcast.9), channel_id=1, replica_groups=mesh['dp'=2,'mp'=16] {'mp'}, use_global_device_ids=true, to_apply=%region_15.16 | all-reduce | flops 3841 | bytes 30728 | tf_op jit(solution)/shard_map/psum | solution.py:47
  358.1 8.4 %all-reduce.1 = (f32[3,1280]{1,0:T(4,128)}, f32[]{:T(128)}) all-reduce(f32[3,1280]{1,0:T(4,128)S(1)} %get-tuple-element.24, f32[]{:T(128)} %get-tuple-element.25), channel_id=1, replica_groups=mesh['dp'=2,'mp'=16] {'dp'}, use_global_device_ids=true, to_apply=%region_16.17 | all-reduce | flops 3841 | bytes 30728 | tf_op jit(solution)/shard_map/psum | solution.py:46
  367.2 0.0 all-to-all-done.1
  367.2 6.1 %copy.22 = f32[1,1280,1024]{2,1,0:T(8,128)} copy(f32[1,1280,1024]{2,0,1:T(1,128)} %all-to-all-done.1) | data formatting | bytes 10485760
  373.4 0.0 all-reduce.4.cloned.1.call-done
  373.4 2.1 copy.17
  (10 shorter events, 0.1 us)
Async XLA Ops:
  7.2 83.9 %all-gather.2.cloned.1.call-start = ((), (), s32[]{:S(2)}) async-start(), calls=%async_computation.3 | async-start | bytes 3481600 | tf_op jit(solution)/shard_map/all_gather | solution.py:29
  7.9 83.1 %all-to-all-start = ((bf16[16,80,1024]{2,1,0:T(8,128)(2,1)}), bf16[16,80,1024]{2,1,0:T(8,128)(2,1)S(1)}, u32[]{:S(2)}, u32[]{:S(2)}) async-start(bf16[16,80,1024]{2,1,0:T(8,128)(2,1)} %param.6), calls=%async_computation | async-start | bytes 5242880 | tf_op jit(solution)/shard_map/all_to_all | solution.py:30
  14.2 286.7 %reduce-scatter.4.cloned.1.call-start = ((), (), s32[]{:S(2)}) async-start(), calls=%async_computation.5 | async-start | bytes 6963200
  98.3 3.9 %copy-start = (f32[1280]{0:T(1024)S(1)}, f32[1280]{0:T(1024)}, u32[]{:S(2)}) copy-start(f32[1280]{0:T(1024)} %param.9) | copy-start | bytes 15364
  98.3 3.9 %copy-start.1 = (f32[1280]{0:T(1024)S(1)}, f32[1280]{0:T(1024)}, u32[]{:S(2)}) copy-start(f32[1280]{0:T(1024)} %param.8) | copy-start | bytes 15364
  98.7 7.7 %copy-start.2 = (f32[1280]{0:T(1024)S(1)}, f32[1280]{0:T(1024)}, u32[]{:S(2)}) copy-start(f32[1280]{0:T(1024)} %param.10) | copy-start | bytes 15364
  161.3 205.9 %all-to-all-start.1 = ((f32[1,1280,1024]{2,0,1:T(1,128)}), f32[1,1280,1024]{2,0,1:T(1,128)}, u32[]{:S(2)}, u32[]{:S(2)}) async-start(f32[1,1280,1024]{2,0,1:T(1,128)} %copy.16), calls=%async_computation.1 | async-start | bytes 10485760 | tf_op jit(solution)/shard_map/all_to_all | solution.py:40
  167.7 205.7 %all-reduce.4.cloned.1.call-start = ((), (), s32[]{:S(2)}) async-start(), calls=%async_computation.4 | async-start | bytes 1310720 | tf_op jit(solution)/shard_map/psum | solution.py:44
Sparse Core Ops, SparseCore 0:
  10.3 75.0 all-gather.1
  137.4 163.3 reduce-scatter.3
  303.2 30.4 all-reduce.3
